TPU v7x, 32 devices: a whole 2x2x4 slice. The times are simulated.
32 devices in a mesh: dp: 16 (over z, y, x), member: 2 (over core).
Axes of the slice: x: 2, y: 2, z: 4, core: 2. Of those that a mesh axis runs over, the one named last changes fastest.
Arguments:
- inputs: bfloat16 [24576, 393], P(('dp', 'member')), may hold values from -256 to 256
- targets: bfloat16 [24576, 377], P(('dp', 'member')), may hold values from -6 to 6
- bootstrap: int32 [2, 24576], P('member', 'dp'), may hold values from 0 to 1535
- lower_weight: bfloat16 [2, 393, 1024], P('member'), may hold values from -0.3125 to 0.3125
- lower_shift: float32 [2, 1024], P('member'), may hold values from -3 to 3
- upper_weight: bfloat16 [2, 1024, 377], P('member'), may hold values from -0.1875 to 0.1875
- upper_shift: float32 [2, 377], P('member'), may hold values from -3 to 3
- log_var: float32 [2, 377], P('member'), may hold values from -1 to 1
Outputs:
- lower_grad: float32 [2, 1024, 393], P('member', 'dp')
- bias_grad: float32 [2, 1024], P('member', 'dp')
- upper_grad: float32 [2, 1024, 377], P('member', 'dp')
- offset_grad: float32 [2, 377], P('member')
- noise_grad: float32 [2, 377], P('member')
- member_loss: float32 [2], P('member')
Inputs may be any that keep to these rules, and one draw needn't show every extreme that they name: bootstrap[m, r] is an offset within the aligned block of 1536 rows that holds row r.
All inputs are finite; a program needn't handle non-finite values.
Results may differ from a plain program's by a relative error of at most 0.00076.
Values may be sent and summed in bfloat16 or wider, within the bound.
A program may use at most 64 MiB of HBM per device.

v0:
```python
import jax
import jax.numpy as jnp
from jax import lax
from jax.sharding import PartitionSpec as P

H = 1024


def member_pass(
    picked, goal_rows, lower_weight, lower_shift, upper_weight, upper_shift, log_var, row_count
):
    pre_act = jnp.dot(picked, lower_weight, preferred_element_type=jnp.float32) + lower_shift
    hidden = jax.nn.silu(pre_act).astype(jnp.bfloat16)
    pred_mean = jnp.dot(hidden, upper_weight, preferred_element_type=jnp.float32) + upper_shift
    residual = pred_mean - goal_rows.astype(jnp.float32)
    scaled_err = residual * jnp.exp(-log_var)
    member_loss = 0.5 * jnp.sum(residual * scaled_err + log_var) / row_count
    grad_mean = scaled_err / row_count
    offset_grad = jnp.sum(grad_mean, axis=0)
    noise_grad = 0.5 * jnp.sum(1.0 - residual * scaled_err, axis=0) / row_count
    grad_half = grad_mean.astype(jnp.bfloat16)
    grad_hidden = lax.dot_general(
        grad_half, upper_weight, (((1,), (1,)), ((), ())), preferred_element_type=jnp.float32
    )
    gate_sig = jax.nn.sigmoid(pre_act)
    grad_pre = grad_hidden * gate_sig * (1.0 + pre_act * (1.0 - gate_sig))
    bias_grad = jnp.sum(grad_pre, axis=0)
    pre_half = grad_pre.astype(jnp.bfloat16)
    return (hidden, grad_half, pre_half, bias_grad, offset_grad, noise_grad, member_loss)


def outer_rows(left, right):
    return lax.dot_general(
        left, right, (((0,), (0,)), ((), ())), preferred_element_type=jnp.float32
    )


def feature_stats(inputs):
    values = inputs.astype(jnp.float32)
    row_count = inputs.shape[0] * lax.axis_size("dp") * lax.axis_size("member")
    col_total = lax.psum(jnp.sum(values, axis=0), ("dp", "member"))
    feature_mean = col_total / row_count
    centered = values - feature_mean
    col_spread = lax.psum(jnp.sum(centered * centered, axis=0), ("dp", "member"))
    feature_var = col_spread / row_count
    return (feature_mean, 1.0 / jnp.sqrt(feature_var + 1e-06))


def per_device(
    inputs, targets, bootstrap, lower_weight, lower_shift, upper_weight, upper_shift, log_var
):
    feature_mean, feature_scale = feature_stats(inputs)
    own_rows = ((inputs.astype(jnp.float32) - feature_mean) * feature_scale).astype(jnp.bfloat16)
    row_block, goal_block = (
        lax.all_gather(own_rows, "member", axis=0, tiled=True),
        lax.all_gather(targets, "member", axis=0, tiled=True),
    )
    row_count = goal_block.shape[0]
    pick_row = bootstrap[0]
    picked = row_block[pick_row]
    passes = [
        (picked,)
        + member_pass(
            picked,
            goal_block[pick_row],
            lower_weight[0],
            lower_shift[0],
            upper_weight[0],
            upper_shift[0],
            log_var[0],
            row_count,
        )
    ]
    share = H // lax.axis_size("dp")
    lower_list, upper_list = ([], [])
    picked, hidden, grad_half, pre_half, bias_one, offset_one, noise_one, loss_one = passes[0]

    def upper_term(start, count, hidden=hidden, grad_half=grad_half):
        return outer_rows(hidden, grad_half)

    def lower_term(start, count, pre_half=pre_half, picked=picked):
        return outer_rows(pre_half, picked)

    upper_list.append(
        lax.psum_scatter(
            upper_term(jnp.int32(0), share * lax.axis_size("dp")),
            "dp",
            scatter_dimension=0,
            tiled=True,
        )
    )
    lower_list.append(
        lax.psum_scatter(
            lower_term(jnp.int32(0), share * lax.axis_size("dp")),
            "dp",
            scatter_dimension=0,
            tiled=True,
        )
    )
    lower_grad = jnp.stack(lower_list)
    upper_grad = jnp.stack(upper_list)
    bias_sum = jnp.stack([item[4] for item in passes])
    offset_sum = jnp.stack([item[5] for item in passes])
    noise_sum = jnp.stack([item[6] for item in passes])
    loss_sum = jnp.stack([item[7] for item in passes])
    bias_total, offset_grad, noise_grad, member_loss = lax.psum(
        (bias_sum, offset_sum, noise_sum, loss_sum), "dp"
    )
    bias_grad = lax.dynamic_slice_in_dim(bias_total, lax.axis_index("dp") * share, share, 1)
    return (lower_grad, bias_grad, upper_grad, offset_grad, noise_grad, member_loss)


def solution(mesh):
    return jax.shard_map(
        per_device,
        mesh=mesh,
        in_specs=(
            P(("dp", "member"), None),
            P(("dp", "member"), None),
            P("member", "dp"),
            P("member", None, None),
            P("member", None),
            P("member", None, None),
            P("member", None),
            P("member", None),
        ),
        out_specs=(
            P("member", "dp", None),
            P("member", "dp"),
            P("member", "dp", None),
            P("member", None),
            P("member", None),
            P("member"),
        ),
        check_vma=False,
    )
```

profile of v0, /device:TPU:0, one launch (start us, length us, event | category | flops | bytes accessed | tf_op | source)
XLA Modules:
  0.0 339.9 jit_solution(8934908891919403699)
XLA Ops:
  7.2 0.0 copy-start
  7.2 0.0 all-gather.5.cloned.1.call-start
  7.2 0.7 all-gather.5.cloned.1.call-update
  7.9 0.0 copy-start.3
  7.9 0.0 copy-start.2
  7.9 0.0 copy-start.4
  7.9 0.0 all-gather.3.cloned.1.call-start
  8.0 1.3 copy.15
  9.3 0.2 convert_reduce_fusion
  9.5 42.0 %psum.42 = f32[393]{0:T(512)S(1)} all-reduce(f32[393]{0:T(512)S(1)} %convert_reduce_fusion), channel_id=1, replica_groups=mesh['dp'=16,'member'=2] {'dp','member'}, use_global_device_ids=true, to_apply=%region_1.0 | all-reduce | flops 393 | bytes 3144 | tf_op jit(solution)/shard_map/psum | solution.py:41
  51.5 0.3 fusion.7
  51.8 40.1 %psum.43 = f32[393]{0:T(512)S(1)} all-reduce(f32[393]{0:T(512)S(1)} %fusion.7), channel_id=1, replica_groups=mesh['dp'=16,'member'=2] {'dp','member'}, use_global_device_ids=true, to_apply=%region_3.0 | all-reduce | flops 393 | bytes 3144 | tf_op jit(solution)/shard_map/psum | solution.py:44
  91.9 1.1 fusion.8
  93.0 0.0 all-gather.3.cloned.1.call-update
  93.0 0.0 reduce-scatter.5.cloned.1.call-start
  93.1 0.0 copy-done.3
  93.1 0.0 copy-done.2
  93.2 0.0 copy-done.4
  93.2 0.0 all-gather.5.cloned.1.call-done
  93.2 6.4 %gather_fusion.1 = bf16[1536,377]{1,0:T(8,128)(2,1)} fusion(bf16[1536,377]{1,0:T(8,128)(2,1)} %all-gather.5.cloned.1.call-done, s32[2048]{0:T(1024)S(1)} %pad_clamp_fusion), kind=kCustom, calls=%fused_computation.1 | custom fusion | bytes 2322432 | tf_op jit(solution)/shard_map/gather | solution.py:65
  99.7 0.0 copy-start.6
  99.7 3.9 %all-gather.3.cloned.1.call-done = bf16[1536,393]{1,0:T(8,128)(2,1)} async-done(((bf16[768,393]{1,0:T(8,128)(2,1)}), bf16[1536,393]{1,0:T(8,128)(2,1)}) %all-gather.3.cloned.1.call-update) | async-done | bytes 1207312 | tf_op jit(solution)/shard_map/all_gather | solution.py:55
  103.6 6.5 %gather_fusion = bf16[1536,393]{1,0:T(8,128)(2,1)S(1)} fusion(bf16[1536,393]{1,0:T(8,128)(2,1)} %all-gather.3.cloned.1.call-done, s32[2048]{0:T(1024)S(1)} %pad_clamp_fusion), kind=kCustom, calls=%fused_computation | custom fusion | bytes 2420736 | tf_op jit(solution)/shard_map/gather | solution.py:60
  110.1 0.0 copy-done
  110.1 0.0 copy-done.6
  110.1 0.0 copy-start.1
  110.1 0.0 copy-start.5
  110.1 5.1 %multiply_convert_fusion = (bf16[1536,1024]{1,0:T(8,128)(2,1)S(1)}, f32[1536,1024]{1,0:T(8,128)}) fusion(f32[1024]{0:T(1024)S(1)} %bitcast.29, bf16[1536,393]{1,0:T(8,128)(2,1)S(1)} %gather_fusion, bf16[1,393,1024]{2,1,0:T(8,128)(2,1)S(1)} %copy-done), kind=kOutput, calls=%fused_computation.3 | convolution fusion | flops 1245708288 | bytes 11453440 | tf_op jit(solution)/shard_map/dot_general | solution.py:12
  115.2 0.0 copy-done.1
  115.2 0.0 copy-done.5
  115.2 3.2 add_reduce_fusion
  118.4 0.0 copy-start.7
  118.4 1.4 copy-done.7
  119.8 3.0 fusion.13
  122.8 0.0 reduce-scatter.5.cloned.1.call-update
  122.9 0.2 reduce-scatter.3.cloned.1.call-start
  123.1 6.4 %fusion.20 = (f32[1024]{0:T(1024)S(1)}, bf16[1536,1024]{1,0:T(8,128)(2,1)S(1)}) fusion(f32[1536,1024]{1,0:T(8,128)} %get-tuple-element.16, f32[1024]{0:T(1024)S(1)} %bitcast.30, bf16[1,1024,377]{2,1,0:T(8,128)(2,1)S(1)} %copy-done.5, f32[1536,377]{1,0:T(8,128)} %copy-done.7, f32[377]{0:T(512)S(1)} %get-tuple-element.10), kind=kOutput, calls=%fused_computation.37 | convolution fusion | flops 1204977152 | bytes 12535268 | tf_op jit(solution)/shard_map/dot_general | solution.py:22
  129.5 3.2 fusion
  132.7 0.0 reduce-scatter.3.cloned.1.call-update
  133.4 43.6 %all-reduce = (f32[1,1024]{1,0:T(1,128)S(1)}, f32[1,377]{1,0:T(1,128)}, f32[1,377]{1,0:T(1,128)}, f32[1]{0:T(128)}) all-reduce(f32[1,1024]{1,0:T(1,128)S(1)} %bitcast.26, f32[1,377]{1,0:T(1,128)S(1)} %stack.19, f32[1,377]{1,0:T(1,128)S(1)} %div.37, f32[1]{0:T(128)} %bitcast.7), channel_id=1, replica_groups=mesh['dp'=16,'member'=2] {'dp'}, use_global_device_ids=true, to_apply=%region_6.7 | all-reduce | flops 1779 | bytes 14232 | tf_op jit(solution)/shard_map/psum | solution.py:106
  177.0 0.6 constant_dynamic-slice_fusion
  177.6 72.6 %reduce-scatter.5.cloned.1.call-done = f32[64,377]{1,0:T(8,128)} async-done(((f32[1024,377]{1,0:T(8,128)}), f32[64,377]{1,0:T(8,128)}) %reduce-scatter.5.cloned.1.call-update) | async-done | bytes 96528 | tf_op jit(solution)/shard_map/reduce_scatter | solution.py:85
  250.3 83.1 %reduce-scatter.3.cloned.1.call-done = f32[64,393]{1,0:T(8,128)} async-done(((f32[1024,393]{1,0:T(8,128)}), f32[64,393]{1,0:T(8,128)}) %reduce-scatter.3.cloned.1.call-update) | async-done | bytes 100624 | tf_op jit(solution)/shard_map/reduce_scatter | solution.py:93
  (9 shorter events, 0.1 us)
Async XLA Ops:
  7.2 102.9 %copy-start = (bf16[1,393,1024]{2,1,0:T(8,128)(2,1)S(1)}, bf16[1,393,1024]{2,1,0:T(8,128)(2,1)}, u32[]{:S(2)}) copy-start(bf16[1,393,1024]{2,1,0:T(8,128)(2,1)} %param.11) | copy-start | bytes 2414596
  7.2 86.0 %all-gather.5.cloned.1.call-start = ((), (), s32[]{:S(2)}) async-start(), calls=%async_computation.3 | async-start | bytes 1769472 | tf_op jit(solution)/shard_map/all_gather | solution.py:56
  7.9 85.2 %copy-start.3 = (f32[1,377]{1,0:T(1,128)S(1)}, f32[1,377]{1,0:T(1,128)}, u32[]{:S(2)}) copy-start(f32[1,377]{1,0:T(1,128)} %param.14) | copy-start | bytes 4528
  7.9 85.2 %copy-start.2 = (s32[1,1536]{1,0:T(1,128)S(1)}, s32[1,1536]{1,0:T(1,128)}, u32[]{:S(2)}) copy-start(s32[1,1536]{1,0:T(1,128)} %param.10) | copy-start | bytes 18436
  7.9 85.2 %copy-start.4 = (f32[1,377]{1,0:T(1,128)S(1)}, f32[1,377]{1,0:T(1,128)}, u32[]{:S(2)}) copy-start(f32[1,377]{1,0:T(1,128)} %param.15) | copy-start | bytes 4528
  7.9 95.6 %all-gather.3.cloned.1.call-start = ((), (), s32[]{:S(2)}) async-start(), calls=%async_computation.2 | async-start | bytes 2359296 | tf_op jit(solution)/shard_map/all_gather | solution.py:55
  93.0 157.2 %reduce-scatter.5.cloned.1.call-start = ((), (), s32[]{:S(2)}) async-start(), calls=%async_computation.5 | async-start | bytes 1671168 | tf_op jit(solution)/shard_map/reduce_scatter | solution.py:85
  99.7 10.4 %copy-start.6 = (f32[1,1024]{1,0:T(1,128)S(1)}, f32[1,1024]{1,0:T(1,128)}, u32[]{:S(2)}) copy-start(f32[1,1024]{1,0:T(1,128)} %param.12) | copy-start | bytes 12292
  110.1 5.1 %copy-start.1 = (bf16[1536,377]{1,0:T(8,128)(2,1)S(1)}, bf16[1536,377]{1,0:T(8,128)(2,1)}, u32[]{:S(2)}) copy-start(bf16[1536,377]{1,0:T(8,128)(2,1)} %gather_fusion.1) | copy-start | bytes 3474436
  110.1 5.1 %copy-start.5 = (bf16[1,1024,377]{2,1,0:T(8,128)(2,1)S(1)}, bf16[1,1024,377]{2,1,0:T(8,128)(2,1)}, u32[]{:S(2)}) copy-start(bf16[1,1024,377]{2,1,0:T(8,128)(2,1)} %param.13) | copy-start | bytes 2316292
  118.4 1.4 copy-start.7
  122.9 210.5 %reduce-scatter.3.cloned.1.call-start = ((), (), s32[]{:S(2)}) async-start(), calls=%async_computation.4 | async-start | bytes 2228224 | tf_op jit(solution)/shard_map/reduce_scatter | solution.py:93
Sparse Core Ops, SparseCore 0:
  9.5 11.9 all-gather.4
  93.1 10.3 all-gather.2
  123.0 127.2 reduce-scatter.4
  253.0 80.3 reduce-scatter.2
where the time goes:
time: 340 us
  waiting for transfers between devices  160 us (47%)
  blocking collectives  126 us (37%)
  matrix products  20.9 us (6%)
  local copies, waits for them, and re-layouts  16.3 us (5%)
  between operations  14.6 us (4%)
    reduce_scatter x1, waiting for transfers between devices, per_device(): lax.psum_scatter(lower_term(jnp.int32(0), share * lax.axis_size('dp')), '...  83.1 us
    reduce_scatter x1, waiting for transfers between devices, per_device(): lax.psum_scatter(upper_term(jnp.int32(0), share * lax.axis_size('dp')), '...  72.6 us
    psum x1, blocking collectives, per_device(): lax.psum((bias_sum, offset_sum, noise_sum, loss_sum), 'dp')  43.6 us
    psum x1, blocking collectives, feature_stats(): col_total = lax.psum(jnp.sum(values, axis=0), ('dp', 'member'))  42 us
    psum x1, blocking collectives, feature_stats(): lax.psum(jnp.sum(centered * centered, axis=0), ('dp', 'member'))  40.1 us
  transfers between devices with their start and end apart: 4, of which 3 were waited for; matrix products, arithmetic and copies ran while one was open for 6% of the time, Pallas kernels for 0%

commit v1 on v0

--- a/solution.py
+++ b/solution.py
@@ -38,7 +38,8 @@
 def feature_stats(inputs):
     values = inputs.astype(jnp.float32)
     row_count = inputs.shape[0] * lax.axis_size("dp") * lax.axis_size("member")
-    col_total = lax.psum(jnp.sum(values, axis=0), ("dp", "member"))
+    one_axis = lax.psum(jnp.sum(values, axis=0), "member")
+    col_total = lax.psum(one_axis, "dp")
     feature_mean = col_total / row_count
     centered = values - feature_mean
     col_spread = lax.psum(jnp.sum(centered * centered, axis=0), ("dp", "member"))

time: 340 us -> 341 us (level)
    psum x1 -> x2, blocking collectives: 42 us -> 46 us  [the longest x1 43.3 us: feature_stats(): col_total = lax.psum(one_axis, 'dp')]
where the time goes in v1:
time: 341 us; the launch traced here: 340 us
  waiting for transfers between devices  160 us (47%)
  blocking collectives  126 us (37%)
  matrix products  20.9 us (6%)
  local copies, waits for them, and re-layouts  16.3 us (5%)
  between operations  14.6 us (4%)
    reduce_scatter x1, waiting for transfers between devices, per_device(): lax.psum_scatter(lower_term(jnp.int32(0), share * lax.axis_size('dp')), '...  83.3 us
    reduce_scatter x1, waiting for transfers between devices, per_device(): lax.psum_scatter(upper_term(jnp.int32(0), share * lax.axis_size('dp')), '...  72.5 us
    psum x1, blocking collectives, per_device(): lax.psum((bias_sum, offset_sum, noise_sum, loss_sum), 'dp')  43.7 us
    psum x1, blocking collectives, feature_stats(): col_total = lax.psum(one_axis, 'dp')  43.3 us
    psum x1, blocking collectives, feature_stats(): lax.psum(jnp.sum(centered * centered, axis=0), ('dp', 'member'))  36.9 us
  transfers between devices with their start and end apart: 4, of which 3 were waited for; matrix products, arithmetic and copies ran while one was open for 6% of the time, Pallas kernels for 0%

profile of v1, /device:TPU:0, one launch (start us, length us, event | category | flops | bytes accessed | tf_op | source)
XLA Modules:
  0.0 340.5 jit_solution(1131835604942940178)
XLA Ops:
  7.2 0.0 copy-start
  7.2 0.0 all-gather.5.cloned.1.call-start
  7.2 0.7 all-gather.5.cloned.1.call-update
  7.9 0.0 copy-start.3
  7.9 0.0 copy-start.2
  7.9 0.0 copy-start.4
  7.9 0.0 all-gather.3.cloned.1.call-start
  8.0 1.3 copy.15
  9.3 0.2 convert_reduce_fusion
  9.5 2.6 psum.49
  12.1 43.3 %psum.50 = f32[393]{0:T(512)S(1)} all-reduce(f32[393]{0:T(512)S(1)} %psum.49), channel_id=1, replica_groups=mesh['dp'=16,'member'=2] {'dp'}, use_global_device_ids=true, to_apply=%region_2.0 | all-reduce | flops 393 | bytes 3144 | tf_op jit(solution)/shard_map/psum | solution.py:42
  55.5 0.3 fusion.7
  55.7 36.9 %psum.51 = f32[393]{0:T(512)S(1)} all-reduce(f32[393]{0:T(512)S(1)} %fusion.7), channel_id=1, replica_groups=mesh['dp'=16,'member'=2] {'dp','member'}, use_global_device_ids=true, to_apply=%region_4.0 | all-reduce | flops 393 | bytes 3144 | tf_op jit(solution)/shard_map/psum | solution.py:45
  92.6 1.1 fusion.8
  93.7 0.0 all-gather.3.cloned.1.call-update
  93.7 0.0 reduce-scatter.5.cloned.1.call-start
  93.8 0.0 copy-done.3
  93.8 0.0 copy-done.2
  93.8 0.0 copy-done.4
  93.9 0.0 all-gather.5.cloned.1.call-done
  93.9 6.4 %gather_fusion.1 = bf16[1536,377]{1,0:T(8,128)(2,1)} fusion(bf16[1536,377]{1,0:T(8,128)(2,1)} %all-gather.5.cloned.1.call-done, s32[2048]{0:T(1024)S(1)} %pad_clamp_fusion), kind=kCustom, calls=%fused_computation.1 | custom fusion | bytes 2322432 | tf_op jit(solution)/shard_map/gather | solution.py:66
  100.4 0.0 copy-start.6
  100.4 3.7 %all-gather.3.cloned.1.call-done = bf16[1536,393]{1,0:T(8,128)(2,1)} async-done(((bf16[768,393]{1,0:T(8,128)(2,1)}), bf16[1536,393]{1,0:T(8,128)(2,1)}) %all-gather.3.cloned.1.call-update) | async-done | bytes 1207312 | tf_op jit(solution)/shard_map/all_gather | solution.py:56
  104.1 6.5 %gather_fusion = bf16[1536,393]{1,0:T(8,128)(2,1)S(1)} fusion(bf16[1536,393]{1,0:T(8,128)(2,1)} %all-gather.3.cloned.1.call-done, s32[2048]{0:T(1024)S(1)} %pad_clamp_fusion), kind=kCustom, calls=%fused_computation | custom fusion | bytes 2420736 | tf_op jit(solution)/shard_map/gather | solution.py:61
  110.6 0.0 copy-done
  110.6 0.0 copy-done.6
  110.6 0.0 copy-start.1
  110.6 0.0 copy-start.5
  110.6 5.0 %multiply_convert_fusion = (bf16[1536,1024]{1,0:T(8,128)(2,1)S(1)}, f32[1536,1024]{1,0:T(8,128)}) fusion(f32[1024]{0:T(1024)S(1)} %bitcast.29, bf16[1536,393]{1,0:T(8,128)(2,1)S(1)} %gather_fusion, bf16[1,393,1024]{2,1,0:T(8,128)(2,1)S(1)} %copy-done), kind=kOutput, calls=%fused_computation.3 | convolution fusion | flops 1245708288 | bytes 11453440 | tf_op jit(solution)/shard_map/dot_general | solution.py:12
  115.7 0.0 copy-done.1
  115.7 0.0 copy-done.5
  115.7 3.2 add_reduce_fusion
  118.9 0.0 copy-start.7
  118.9 1.4 copy-done.7
  120.3 3.0 fusion.13
  123.3 0.0 reduce-scatter.5.cloned.1.call-update
  123.4 0.2 reduce-scatter.3.cloned.1.call-start
  123.6 6.4 %fusion.20 = (f32[1024]{0:T(1024)S(1)}, bf16[1536,1024]{1,0:T(8,128)(2,1)S(1)}) fusion(f32[1536,1024]{1,0:T(8,128)} %get-tuple-element.16, f32[1024]{0:T(1024)S(1)} %bitcast.30, bf16[1,1024,377]{2,1,0:T(8,128)(2,1)S(1)} %copy-done.5, f32[1536,377]{1,0:T(8,128)} %copy-done.7, f32[377]{0:T(512)S(1)} %get-tuple-element.10), kind=kOutput, calls=%fused_computation.37 | convolution fusion | flops 1204977152 | bytes 12535268 | tf_op jit(solution)/shard_map/dot_general | solution.py:22
  130.0 3.2 fusion
  133.2 0.0 reduce-scatter.3.cloned.1.call-update
  133.9 43.7 %all-reduce = (f32[1,1024]{1,0:T(1,128)S(1)}, f32[1,377]{1,0:T(1,128)}, f32[1,377]{1,0:T(1,128)}, f32[1]{0:T(128)}) all-reduce(f32[1,1024]{1,0:T(1,128)S(1)} %bitcast.26, f32[1,377]{1,0:T(1,128)S(1)} %stack.19, f32[1,377]{1,0:T(1,128)S(1)} %div.37, f32[1]{0:T(128)} %bitcast.7), channel_id=1, replica_groups=mesh['dp'=16,'member'=2] {'dp'}, use_global_device_ids=true, to_apply=%region_7.8 | all-reduce | flops 1779 | bytes 14232 | tf_op jit(solution)/shard_map/psum | solution.py:107
  177.6 0.6 constant_dynamic-slice_fusion
  178.2 72.5 %reduce-scatter.5.cloned.1.call-done = f32[64,377]{1,0:T(8,128)} async-done(((f32[1024,377]{1,0:T(8,128)}), f32[64,377]{1,0:T(8,128)}) %reduce-scatter.5.cloned.1.call-update) | async-done | bytes 96528 | tf_op jit(solution)/shard_map/reduce_scatter | solution.py:86
  250.7 83.3 %reduce-scatter.3.cloned.1.call-done = f32[64,393]{1,0:T(8,128)} async-done(((f32[1024,393]{1,0:T(8,128)}), f32[64,393]{1,0:T(8,128)}) %reduce-scatter.3.cloned.1.call-update) | async-done | bytes 100624 | tf_op jit(solution)/shard_map/reduce_scatter | solution.py:94
  (9 shorter events, 0.1 us)
Async XLA Ops:
  7.2 103.4 %copy-start = (bf16[1,393,1024]{2,1,0:T(8,128)(2,1)S(1)}, bf16[1,393,1024]{2,1,0:T(8,128)(2,1)}, u32[]{:S(2)}) copy-start(bf16[1,393,1024]{2,1,0:T(8,128)(2,1)} %param.11) | copy-start | bytes 2414596
  7.2 86.7 %all-gather.5.cloned.1.call-start = ((), (), s32[]{:S(2)}) async-start(), calls=%async_computation.3 | async-start | bytes 1769472 | tf_op jit(solution)/shard_map/all_gather | solution.py:57
  7.9 85.8 %copy-start.3 = (f32[1,377]{1,0:T(1,128)S(1)}, f32[1,377]{1,0:T(1,128)}, u32[]{:S(2)}) copy-start(f32[1,377]{1,0:T(1,128)} %param.14) | copy-start | bytes 4528
  7.9 85.9 %copy-start.2 = (s32[1,1536]{1,0:T(1,128)S(1)}, s32[1,1536]{1,0:T(1,128)}, u32[]{:S(2)}) copy-start(s32[1,1536]{1,0:T(1,128)} %param.10) | copy-start | bytes 18436
  7.9 85.9 %copy-start.4 = (f32[1,377]{1,0:T(1,128)S(1)}, f32[1,377]{1,0:T(1,128)}, u32[]{:S(2)}) copy-start(f32[1,377]{1,0:T(1,128)} %param.15) | copy-start | bytes 4528
  7.9 96.1 %all-gather.3.cloned.1.call-start = ((), (), s32[]{:S(2)}) async-start(), calls=%async_computation.2 | async-start | bytes 2359296 | tf_op jit(solution)/shard_map/all_gather | solution.py:56
  93.7 157.0 %reduce-scatter.5.cloned.1.call-start = ((), (), s32[]{:S(2)}) async-start(), calls=%async_computation.5 | async-start | bytes 1671168 | tf_op jit(solution)/shard_map/reduce_scatter | solution.py:86
  100.4 10.2 %copy-start.6 = (f32[1,1024]{1,0:T(1,128)S(1)}, f32[1,1024]{1,0:T(1,128)}, u32[]{:S(2)}) copy-start(f32[1,1024]{1,0:T(1,128)} %param.12) | copy-start | bytes 12292
  110.6 5.1 %copy-start.1 = (bf16[1536,377]{1,0:T(8,128)(2,1)S(1)}, bf16[1536,377]{1,0:T(8,128)(2,1)}, u32[]{:S(2)}) copy-start(bf16[1536,377]{1,0:T(8,128)(2,1)} %gather_fusion.1) | copy-start | bytes 3474436
  110.6 5.1 %copy-start.5 = (bf16[1,1024,377]{2,1,0:T(8,128)(2,1)S(1)}, bf16[1,1024,377]{2,1,0:T(8,128)(2,1)}, u32[]{:S(2)}) copy-start(bf16[1,1024,377]{2,1,0:T(8,128)(2,1)} %param.13) | copy-start | bytes 2316292
  118.9 1.4 copy-start.7
  123.4 210.6 %reduce-scatter.3.cloned.1.call-start = ((), (), s32[]{:S(2)}) async-start(), calls=%async_computation.4 | async-start | bytes 2228224 | tf_op jit(solution)/shard_map/reduce_scatter | solution.py:94
Sparse Core Ops, SparseCore 0:
  9.5 11.9 all-gather.4
  93.8 10.2 all-gather.2
  123.5 127.1 reduce-scatter.4
  253.4 80.5 reduce-scatter.2
